TPU v7x, 32 devices: a whole 2x2x4 slice. The times are simulated.
32 devices in a mesh: rep: 4 (over z), seq: 8 (over y, x, core).
Axes of the slice: x: 2, y: 2, z: 4, core: 2. Of those that a mesh axis runs over, the one named last changes fastest.
Arguments:
- frames_in: bfloat16 [4, 8, 4, 128, 1152], P('rep', 'seq'), may hold values from -6 to 6
- conditioning: float32 [4, 1152], P('rep'), may hold values from -6 to 6
- mod_first: bfloat16 [1152, 6912], P('seq'), may hold values from -0.1875 to 0.1875
- qkv_first: bfloat16 [1152, 3456], P('seq'), may hold values from -0.1875 to 0.1875
- out_first: bfloat16 [1152, 1152], P('seq'), may hold values from -0.75 to 0.75
- up_first: bfloat16 [1152, 4608], P('seq'), may hold values from -0.1875 to 0.1875
- down_first: bfloat16 [4608, 1152], P('seq'), may hold values from -0.09375 to 0.09375
- mod_second: bfloat16 [1152, 6912], P('seq'), may hold values from -0.1875 to 0.1875
- qkv_second: bfloat16 [1152, 3456], P('seq'), may hold values from -0.1875 to 0.1875
- out_second: bfloat16 [1152, 1152], P('seq'), may hold values from -0.375 to 0.375
- up_second: bfloat16 [1152, 4608], P('seq'), may hold values from -0.1875 to 0.1875
- down_second: bfloat16 [4608, 1152], P('seq'), may hold values from -0.09375 to 0.09375
- cotangent: float32 [4, 8, 4, 128, 1152], P('rep', 'seq'), may hold values from -6 to 6
Outputs:
- block_out: float32 [4, 8, 4, 128, 1152], P('rep', 'seq')
- input_grad: float32 [4, 8, 4, 128, 1152], P('rep', 'seq')
- conditioning_grad: float32 [4, 1152], P('rep', 'seq')
- mod_first_grad: float32 [1152, 6912], P('seq')
- qkv_first_grad: float32 [1152, 3456], P('seq')
- out_first_grad: float32 [1152, 1152], P('seq')
- up_first_grad: float32 [1152, 4608], P('seq')
- first_down_gradient: float32 [4608, 1152], P('seq')
- mod_second_grad: float32 [1152, 6912], P('seq')
- qkv_second_grad: float32 [1152, 3456], P('seq')
- out_second_grad: float32 [1152, 1152], P('seq')
- up_second_grad: float32 [1152, 4608], P('seq')
- down_second_grad: float32 [4608, 1152], P('seq')
All inputs are finite; a program needn't handle non-finite values.
Results may differ from a plain program's by a relative error of at most 0.02175.
Values may be sent and summed in bfloat16 or wider, within the bound.
A program may use at most 384 MiB of HBM per device.

v0:
```python
import jax
import jax.numpy as jnp
from jax import lax
from jax.sharding import PartitionSpec as P

HEADS = 16
HEAD_WIDTH = 72
norm_epsilon = 1e-06


def from_partner(block, axis, apart):
    count = lax.axis_size(axis)
    route = []
    for low in range(count):
        high = low | 1 << apart
        if high != low and high < count:
            route += [(low, high), (high, low)]
    return lax.ppermute(block, axis, route)


def shortened(x):
    return jax.tree.map(lambda a: a.astype(jnp.bfloat16) if a.dtype == jnp.float32 else a, x)


def layer_mod(stream, shift_part, scale_part):
    row_mean = jnp.mean(stream, axis=-1, keepdims=True)
    centred = stream - row_mean
    row_var = jnp.mean(centred * centred, axis=-1, keepdims=True)
    return centred * lax.rsqrt(row_var + norm_epsilon) * (1.0 + scale_part) + shift_part


def gelu_tanh(pre_value):
    return jax.nn.gelu(pre_value, approximate=True)


def project(left_operand, right_operand):
    return jnp.einsum(
        "csld,de->csle", left_operand, right_operand, preferred_element_type=jnp.float32
    )


def project_back(incoming, right_operand):
    return jnp.einsum("csle,de->csld", incoming, right_operand, preferred_element_type=jnp.float32)


def mod_parts(modulation):
    return [segment[:, None, None, :] for segment in jnp.split(modulation, 6, axis=-1)]


def modulations(conditioning, mod_one, mod_two):
    row_count = mod_one.shape[0]
    row_start = lax.axis_index("seq") * row_count
    silu_local = lax.dynamic_slice_in_dim(
        jax.nn.silu(conditioning), row_start, row_count, 1
    ).astype(jnp.bfloat16)
    part_one = jnp.dot(silu_local, mod_one, preferred_element_type=jnp.float32)
    part_two = jnp.dot(silu_local, mod_two, preferred_element_type=jnp.float32)
    summed = lax.psum((part_one, part_two), "seq")
    return (summed[0], summed[1], silu_local, row_start)


def gather_layer(qkv_w, out_w, up_w, down_w):
    return (
        lax.all_gather(qkv_w, "seq", axis=0, tiled=True),
        lax.all_gather(out_w, "seq", axis=0, tiled=True),
        lax.all_gather(up_w, "seq", axis=0, tiled=True),
        lax.all_gather(down_w, "seq", axis=0, tiled=True),
    )


def gather_layer_again(qkv_w, out_w, up_w, down_w):
    return (
        lax.all_gather(qkv_w, "seq", axis=0, tiled=True),
        lax.all_gather(out_w, "seq", axis=0, tiled=True),
        lax.all_gather(up_w, "seq", axis=0, tiled=True),
        lax.all_gather(down_w, "seq", axis=0, tiled=True),
    )


def partner_values(stacked):
    return from_partner(stacked, "seq", 0)


def partner_grads(stacked):
    return from_partner(stacked.astype(jnp.bfloat16), "seq", 0).astype(stacked.dtype)


def to_places(stream):
    clip_count, frame_dev, half_places, features = stream.shape
    devices = lax.axis_size("seq")
    place_part = half_places // devices
    exchanged = lax.all_to_all(
        stream.reshape(1, clip_count, frame_dev, devices, place_part, features).astype(
            jnp.bfloat16
        ),
        "seq",
        split_axis=3,
        concat_axis=0,
        tiled=True,
    ).astype(jnp.float32)
    exchanged = exchanged.reshape(devices // 2, 2, clip_count, frame_dev, place_part, features)
    exchanged = jnp.transpose(exchanged, (2, 1, 4, 0, 3, 5))
    return exchanged.reshape(clip_count, 2 * place_part, devices // 2 * frame_dev, features)


def to_frames(stream, frame_dev):
    clip_count, place_count, frame_total, features = stream.shape
    devices = lax.axis_size("seq")
    place_part = place_count // 2
    arranged = stream.reshape(clip_count, 2, place_part, devices // 2, frame_dev, features)
    arranged = jnp.transpose(arranged, (3, 1, 0, 4, 2, 5)).reshape(
        devices, clip_count, frame_dev, 1, place_part, features
    )
    exchanged = lax.all_to_all(
        shortened(arranged), "seq", split_axis=0, concat_axis=3, tiled=True
    ).astype(arranged.dtype)
    return exchanged.reshape(clip_count, frame_dev, devices * place_part, features)


def forward_layer(stream, modulation, weights, spatial):
    qkv_w, out_w, up_w, down_w = weights
    shift_attn, scale_attn, gate_attn, shift_mlp, scale_mlp, gate_mlp = mod_parts(modulation)
    clip_count, seq_count, seq_len, features = stream.shape
    normed = layer_mod(stream, shift_attn, scale_attn).astype(jnp.bfloat16)
    projected = project(normed, qkv_w).astype(jnp.bfloat16)
    queries, keys_all, values_all = jnp.split(projected, 3, axis=-1)
    if spatial:
        remote = partner_values(jnp.stack([keys_all, values_all]))
        keys_all = jnp.concatenate([keys_all, remote[0]], axis=2)
        values_all = jnp.concatenate([values_all, remote[1]], axis=2)
    key_len = keys_all.shape[2]
    queries = queries.reshape(clip_count, seq_count, seq_len, HEADS, HEAD_WIDTH)
    keys_all = keys_all.reshape(clip_count, seq_count, key_len, HEADS, HEAD_WIDTH)
    values_all = values_all.reshape(clip_count, seq_count, key_len, HEADS, HEAD_WIDTH)
    scores = jnp.einsum(
        "cslhe,csmhe->cshlm", queries, keys_all, preferred_element_type=jnp.float32
    ) * HEAD_WIDTH ** (-0.5)
    peak_score = jnp.max(scores, axis=-1, keepdims=True)
    scaled_exp = jnp.exp(scores - peak_score)
    attention = scaled_exp / jnp.sum(scaled_exp, axis=-1, keepdims=True)
    attention_low = attention.astype(jnp.bfloat16)
    attended = jnp.einsum(
        "cshlm,csmhe->cslhe", attention_low, values_all, preferred_element_type=jnp.float32
    )
    attended = attended.astype(jnp.bfloat16).reshape(clip_count, seq_count, seq_len, features)
    branch = project(attended, out_w)
    middle = stream + gate_attn * branch
    normed_mid = layer_mod(middle, shift_mlp, scale_mlp).astype(jnp.bfloat16)
    hidden_pre = project(normed_mid, up_w)
    hidden = gelu_tanh(hidden_pre).astype(jnp.bfloat16)
    mlp_out = project(hidden, down_w)
    result = middle + gate_mlp * mlp_out
    kept_state = (
        normed,
        queries,
        keys_all,
        values_all,
        attention,
        attention_low,
        attended,
        branch,
        middle,
        normed_mid,
        hidden_pre,
        hidden,
        mlp_out,
    )
    return (result, kept_state)


def backward_layer(result_grad, stream, modulation, weights, kept_state, spatial):
    qkv_w, out_w, up_w, down_w = weights
    (
        normed,
        queries,
        keys_all,
        values_all,
        attention,
        attention_low,
        attended,
        branch,
        middle,
        normed_mid,
        hidden_pre,
        hidden,
        mlp_out,
    ) = kept_state
    shift_attn, scale_attn, gate_attn, shift_mlp, scale_mlp, gate_mlp = mod_parts(modulation)
    clip_count, seq_count, seq_len, features = stream.shape
    gate_mlp_grad = jnp.sum(result_grad * mlp_out, axis=(1, 2))
    mlp_grad = (gate_mlp * result_grad).astype(jnp.bfloat16)
    hidden_grad = project_back(mlp_grad, down_w)
    pre_grad = jax.vjp(gelu_tanh, hidden_pre)[1](hidden_grad)[0].astype(jnp.bfloat16)
    normed_mid_grad = project_back(pre_grad, up_w)
    middle_ln_grad, shift_mlp_grad, scale_mlp_grad = jax.vjp(
        layer_mod, middle, shift_mlp, scale_mlp
    )[1](normed_mid_grad)
    middle_grad = result_grad + middle_ln_grad
    gate_attn_grad = jnp.sum(middle_grad * branch, axis=(1, 2))
    branch_grad = (gate_attn * middle_grad).astype(jnp.bfloat16)
    attended_grad = project_back(branch_grad, out_w).astype(jnp.bfloat16)
    attended_grad = attended_grad.reshape(clip_count, seq_count, seq_len, HEADS, HEAD_WIDTH)
    attention_grad = jnp.einsum(
        "cslhe,csmhe->cshlm", attended_grad, values_all, preferred_element_type=jnp.float32
    )
    scores_grad = attention * (
        attention_grad - jnp.sum(attention_grad * attention, axis=-1, keepdims=True)
    )
    scores_grad = scores_grad.astype(jnp.bfloat16)
    inv_root = HEAD_WIDTH ** (-0.5)
    queries_grad = (
        jnp.einsum("cshlm,csmhe->cslhe", scores_grad, keys_all, preferred_element_type=jnp.float32)
        * inv_root
    )
    keys_grad = (
        jnp.einsum("cshlm,cslhe->csmhe", scores_grad, queries, preferred_element_type=jnp.float32)
        * inv_root
    )
    values_grad = jnp.einsum(
        "cshlm,cslhe->csmhe", attention_low, attended_grad, preferred_element_type=jnp.float32
    )
    if spatial:
        returned = partner_grads(
            jnp.stack([keys_grad[:, :, seq_len:], values_grad[:, :, seq_len:]])
        )
        keys_grad = keys_grad[:, :, :seq_len] + returned[0]
        values_grad = values_grad[:, :, :seq_len] + returned[1]
    qkv_grad = jnp.concatenate(
        [
            component.reshape(clip_count, seq_count, seq_len, features)
            for component in (queries_grad, keys_grad, values_grad)
        ],
        axis=-1,
    )
    qkv_grad = qkv_grad.astype(jnp.bfloat16)
    normed_grad = project_back(qkv_grad, qkv_w)
    stream_ln_grad, attention_shift_gradient, scale_attn_grad = jax.vjp(
        layer_mod, stream, shift_attn, scale_attn
    )[1](normed_grad)
    stream_grad = middle_grad + stream_ln_grad
    mod_grad = jnp.concatenate(
        [
            attention_shift_gradient.reshape(clip_count, features),
            scale_attn_grad.reshape(clip_count, features),
            gate_attn_grad,
            shift_mlp_grad.reshape(clip_count, features),
            scale_mlp_grad.reshape(clip_count, features),
            gate_mlp_grad,
        ],
        axis=-1,
    )
    grad_pairs = (
        (normed, qkv_grad),
        (attended, branch_grad),
        (normed_mid, pre_grad),
        (hidden, mlp_grad),
    )
    return (stream_grad, mod_grad, grad_pairs)


def spread_rows_out(left_operand, right_operand):
    left_flat = left_operand.reshape(-1, left_operand.shape[-1])
    right_flat = right_operand.reshape(-1, right_operand.shape[-1])
    return lax.psum_scatter(
        jnp.einsum("nd,ne->de", left_flat, right_flat, preferred_element_type=jnp.float32).astype(
            jnp.bfloat16
        ),
        "seq",
        scatter_dimension=0,
        tiled=True,
    ).astype(jnp.float32)


def layer_grads(grad_pairs):
    return tuple(
        (spread_rows_out(grad_pairs[index][0], grad_pairs[index][1]) for index in range(4))
    )


def per_device(
    frames_in,
    conditioning,
    mod_first,
    qkv_first,
    out_first,
    up_first,
    down_first,
    mod_second,
    qkv_second,
    out_second,
    up_second,
    down_second,
    cotangent,
):
    clip_count = frames_in.shape[0]
    frame_dev = frames_in.shape[2]
    half_places = frames_in.shape[3]
    features = frames_in.shape[4]
    start_stream = frames_in.reshape(clip_count, frame_dev, half_places, features).astype(
        jnp.float32
    )
    mod_one, mod_two, silu_local, row_start = modulations(conditioning, mod_first, mod_second)
    weights_one = gather_layer(qkv_first, out_first, up_first, down_first)
    spatial_out, unused_one = forward_layer(start_stream, mod_one, weights_one, True)
    weights_two = gather_layer(qkv_second, out_second, up_second, down_second)
    temporal_out, unused_two = forward_layer(to_places(spatial_out), mod_two, weights_two, False)
    block_out = to_frames(temporal_out, frame_dev)
    mod_one, mod_two, silu_local, row_start = modulations(conditioning, mod_first, mod_second)
    again_one = gather_layer_again(qkv_first, out_first, up_first, down_first)
    spatial_again, state_one = forward_layer(start_stream, mod_one, again_one, True)
    again_two = gather_layer_again(qkv_second, out_second, up_second, down_second)
    placed_again = to_places(spatial_again)
    unused_three, state_two = forward_layer(placed_again, mod_two, again_two, False)
    cotangent_sites = to_places(cotangent.reshape(clip_count, frame_dev, half_places, features))
    placed_grad, mod_grad_two, pairs_two = backward_layer(
        cotangent_sites, placed_again, mod_two, again_two, state_two, False
    )
    row_attn = qkv_first.shape[0]
    grads_two = layer_grads(pairs_two)
    spatial_grad = to_frames(placed_grad, frame_dev)
    stream_grad, mod_grad_one, pairs_one = backward_layer(
        spatial_grad, start_stream, mod_one, again_one, state_one, True
    )
    grads_one = layer_grads(pairs_one)
    mod_totals = (
        lax.psum(mod_grad_one.astype(jnp.bfloat16), "seq").astype(jnp.float32),
        lax.psum(mod_grad_two.astype(jnp.bfloat16), "seq").astype(jnp.float32),
    )
    low_one = mod_totals[0].astype(jnp.bfloat16)
    low_two = mod_totals[1].astype(jnp.bfloat16)
    mod_weight_one = jnp.einsum(
        "cd,ce->de", silu_local, low_one, preferred_element_type=jnp.float32
    )
    mod_weight_two = jnp.einsum(
        "cd,ce->de", silu_local, low_two, preferred_element_type=jnp.float32
    )
    silu_grad = jnp.einsum("ce,de->cd", low_one, mod_first, preferred_element_type=jnp.float32)
    silu_grad = silu_grad + jnp.einsum(
        "ce,de->cd", low_two, mod_second, preferred_element_type=jnp.float32
    )
    condition_local = lax.dynamic_slice_in_dim(conditioning, row_start, row_attn, 1)
    condition_grad = jax.vjp(jax.nn.silu, condition_local)[1](silu_grad)[0]
    summed = (
        lax.psum(mod_weight_one.astype(jnp.bfloat16), "rep").astype(jnp.float32),
        lax.psum(grads_one[0].astype(jnp.bfloat16), "rep").astype(jnp.float32),
        lax.psum(grads_one[1].astype(jnp.bfloat16), "rep").astype(jnp.float32),
        lax.psum(grads_one[2].astype(jnp.bfloat16), "rep").astype(jnp.float32),
        lax.psum(grads_one[3].astype(jnp.bfloat16), "rep").astype(jnp.float32),
        lax.psum(mod_weight_two.astype(jnp.bfloat16), "rep").astype(jnp.float32),
        lax.psum(grads_two[0].astype(jnp.bfloat16), "rep").astype(jnp.float32),
        lax.psum(grads_two[1].astype(jnp.bfloat16), "rep").astype(jnp.float32),
        lax.psum(grads_two[2].astype(jnp.bfloat16), "rep").astype(jnp.float32),
        lax.psum(grads_two[3].astype(jnp.bfloat16), "rep").astype(jnp.float32),
    )
    out_shape = (clip_count, 1, frame_dev, half_places, features)
    return (
        block_out.reshape(out_shape),
        stream_grad.reshape(out_shape),
        condition_grad,
        summed[0],
        summed[1],
        summed[2],
        summed[3],
        summed[4],
        summed[5],
        summed[6],
        summed[7],
        summed[8],
        summed[9],
    )


def solution(mesh):
    return jax.shard_map(
        per_device,
        mesh=mesh,
        in_specs=(
            P("rep", "seq", None, None, None),
            P("rep", None),
            P("seq", None),
            P("seq", None),
            P("seq", None),
            P("seq", None),
            P("seq", None),
            P("seq", None),
            P("seq", None),
            P("seq", None),
            P("seq", None),
            P("seq", None),
            P("rep", "seq", None, None, None),
        ),
        out_specs=(
            P("rep", "seq", None, None, None),
            P("rep", "seq", None, None, None),
            P("rep", "seq"),
            P("seq", None),
            P("seq", None),
            P("seq", None),
            P("seq", None),
            P("seq", None),
            P("seq", None),
            P("seq", None),
            P("seq", None),
            P("seq", None),
            P("seq", None),
        ),
        check_vma=False,
    )
```

profile of v0, /device:TPU:0, one launch (start us, length us, event | category | flops | bytes accessed | tf_op | source)
XLA Modules:
  0.0 1629.8 jit_solution(10004412810075176240)
XLA Ops:
  17.6 26.8 %all-reduce = (f32[1,6912]{1,0:T(1,128)S(1)}, f32[1,6912]{1,0:T(1,128)S(1)}) all-reduce(f32[1,6912]{1,0:T(1,128)S(1)} %fusion.149, f32[1,6912]{1,0:T(1,128)S(1)} %fusion.147), channel_id=1, replica_groups=mesh['rep'=4,'seq'=8] {'seq'}, use_global_device_ids=true, to_apply=%region_0.1 | all-reduce | flops 13824 | bytes 110592 | tf_op jit(solution)/shard_map/psum | solution.py:58
  44.6 21.0 %all-gather.9.cloned.1.call-done = bf16[1152,3456]{1,0:T(8,128)(2,1)} async-done(((bf16[144,3456]{1,0:T(8,128)(2,1)}), bf16[1152,3456]{1,0:T(8,128)(2,1)}) %all-gather.9.cloned.1.call-update) | async-done | bytes 7962640 | tf_op jit(solution)/shard_map/all_gather | solution.py:64
  109.1 22.1 %fusion.119 = bf16[4,16,72,128]{3,2,1,0:T(8,128)(2,1)} fusion(bf16[1,4,128,16,72]{2,4,3,1,0:T(8,128)(2,1)} %bitcast.356, bf16[1,4,128,16,72]{2,4,3,1,0:T(8,128)(2,1)} %bitcast.354, f32[4,16,128]{2,1,0:T(8,128)S(1)} %get-tuple-element.81, f32[4,16,128,256]{3,2,1,0:T(8,128)} %copy-done.5), kind=kOutput, calls=%fused_computation.180 | convolution fusion | flops 317792512 | bytes 11960320 | tf_op jit(solution)/shard_map/cshlm,csmhe->cslhe/dot_general | solution.py:142
  138.6 36.5 %all-gather.13.cloned.1.call-done = bf16[1152,4608]{1,0:T(8,128)(2,1)} async-done(((bf16[144,4608]{1,0:T(8,128)(2,1)}), bf16[1152,4608]{1,0:T(8,128)(2,1)}) %all-gather.13.cloned.1.call-update) | async-done | bytes 10616848 | tf_op jit(solution)/shard_map/all_gather | solution.py:66
  175.1 23.9 %fusion.22 = f32[4,128,4608]{2,1,0:T(8,128)} fusion(bf16[1152,4608]{1,0:T(8,128)(2,1)} %all-gather.13.cloned.1.call-done, f32[4,128,1152]{2,1,0:T(8,128)} %copy-done.3, f32[1152]{0:T(1024)S(1)} %get-tuple-element.32, f32[1152]{0:T(1024)S(1)} %get-tuple-element.33, f32[4,128]{1,0:T(4,128)S(1)} %fusion.144, f32[4,128]{1,0:T(4,128)S(1)} %broadcast_multiply_fusion.2), kind=kOutput, calls=%fused_computation.32 | convolution fusion | flops 5438767104 | bytes 22426624 | tf_op jit(solution)/shard_map/csld,de->csle/dot_general | solution.py:37
  199.1 41.6 %all-gather.15.cloned.1.call-done = bf16[4608,1152]{1,0:T(8,128)(2,1)} async-done(((bf16[576,1152]{1,0:T(8,128)(2,1)}), bf16[4608,1152]{1,0:T(8,128)(2,1)}) %all-gather.15.cloned.1.call-update) | async-done | bytes 10616848 | tf_op jit(solution)/shard_map/all_gather | solution.py:67
  240.7 13.8 add_convert_fusion.4
  330.9 16.3 %fusion.179 = (f32[32,16,16]{2,1,0:T(8,128)S(1)}, f32[32,16,16,16]{2,3,1,0:T(8,128)S(1)}) fusion(f32[32,16,16,16]{2,3,1,0:T(8,128)S(1)} %fusion.109), kind=kOutput, calls=%fused_computation.279 | output fusion | flops 524303 | bytes 1081344 | tf_op jit(solution)/shard_map/sub | solution.py:139
  363.9 34.0 %all-gather.21.cloned.1.call-done = bf16[1152,4608]{1,0:T(8,128)(2,1)} async-done(((bf16[144,4608]{1,0:T(8,128)(2,1)}), bf16[1152,4608]{1,0:T(8,128)(2,1)}) %all-gather.21.cloned.1.call-update) | async-done | bytes 10616848 | tf_op jit(solution)/shard_map/all_gather | solution.py:66
  397.9 13.2 fusion.14
  411.1 52.6 %all-gather.23.cloned.1.call-done = bf16[4608,1152]{1,0:T(8,128)(2,1)} async-done(((bf16[576,1152]{1,0:T(8,128)(2,1)}), bf16[4608,1152]{1,0:T(8,128)(2,1)}) %all-gather.23.cloned.1.call-update) | async-done | bytes 10616848 | tf_op jit(solution)/shard_map/all_gather | solution.py:67
  463.7 16.0 fusion.37
  479.6 13.5 multiply_reduce_fusion.13
  497.5 18.1 %multiply_reduce_fusion.4 = (bf16[1152]{0:T(1024)(128)(2,1)}, bf16[32,16,1152]{2,1,0:T(8,128)(2,1)}, bf16[1152]{0:T(1024)(128)(2,1)}, f32[32,16,1152]{2,1,0:T(8,128)S(1)}) fusion(f32[32,16,1152]{2,1,0:T(8,128)} %reshape.1279, f32[32,16,1152]{2,1,0:T(8,128)} %get-tuple-element.59, f32[1152]{0:T(1024)S(1)} %get-tuple-element.25, ...), kind=kOutput, calls=%fused_computation.133 | convolution fusion | flops 5465896960 | bytes 33052160 | tf_op jit(solution)/shard_map/csld,de->csle/dot_general | solution.py:37
  563.1 10.9 multiply_reduce_fusion.12
  606.5 17.4 %fusion.30 = bf16[4,128,4608]{2,1,0:T(8,128)(2,1)} fusion(f32[4,128,4608]{2,1,0:T(8,128)} %fusion.22, bf16[4608,1152]{1,0:T(8,128)(2,1)} %all-gather.15.cloned.1.call-done, f32[4,128,1152]{2,1,0:T(8,128)S(1)} %bitcast.337, f32[1152]{0:T(1024)S(1)} %copy-done.64), kind=kOutput, calls=%fused_computation.40 | convolution fusion | flops 5484183552 | bytes 27136512 | tf_op jit(solution)/shard_map/csle,de->csld/dot_general | solution.py:43
  624.0 11.9 multiply_reduce_fusion.11
  646.3 10.6 fusion.7
  664.3 22.2 %convolution_bitcast_fusion.6 = f32[1,4,256,16,72]{2,4,3,1,0:T(8,128)} fusion(bf16[4,128,16,72]{1,3,2,0:T(8,128)(2,1)} %bitcast.360, f32[4,16,128]{2,1,0:T(8,128)S(1)} %copy-done.54, f32[4,16,128,256]{3,2,1,0:T(8,128)} %copy-done.5), kind=kOutput, calls=%fused_computation.161 | convolution fusion | flops 312484096 | bytes 14319616 | tf_op jit(solution)/shard_map/cshlm,cslhe->csmhe/dot_general | solution.py:219
  732.1 13.0 fusion.3
  745.8 11.2 fusion.2
  758.5 12.1 fusion.5
  771.3 11.5 fusion.4
  784.2 10.9 fusion.85
  797.8 23.5 %all-reduce.1 = (bf16[6912]{0:T(1024)(128)(2,1)S(1)}, bf16[6912]{0:T(1024)(128)(2,1)S(1)}) all-reduce(bf16[6912]{0:T(1024)(128)(2,1)S(1)} %reduce.79, bf16[6912]{0:T(1024)(128)(2,1)S(1)} %reduce.80), channel_id=1, replica_groups=mesh['rep'=4,'seq'=8] {'seq'}, use_global_device_ids=true, to_apply=%region_30.31 | all-reduce | flops 13824 | bytes 55296 | tf_op jit(solution)/shard_map/psum | solution.py:326
  823.8 20.3 %reduce-scatter.9.cloned.1.call-done = bf16[144,3456]{1,0:T(8,128)(2,1)} async-done(((bf16[1152,3456]{1,0:T(8,128)(2,1)}), bf16[144,3456]{1,0:T(8,128)(2,1)}) %reduce-scatter.9.cloned.1.call-update) | async-done | bytes 995344 | tf_op jit(solution)/shard_map/reduce_scatter | solution.py:264
  844.1 85.7 %reduce-scatter.23.cloned.1.call-done = bf16[576,1152]{1,0:T(8,128)(2,1)} async-done(((bf16[4608,1152]{1,0:T(8,128)(2,1)}), bf16[576,1152]{1,0:T(8,128)(2,1)}) %reduce-scatter.23.cloned.1.call-update) | async-done | bytes 1327120 | tf_op jit(solution)/shard_map/reduce_scatter | solution.py:264
  929.8 85.6 %reduce-scatter.21.cloned.1.call-done = bf16[144,4608]{1,0:T(8,128)(2,1)} async-done(((bf16[1152,4608]{1,0:T(8,128)(2,1)}), bf16[144,4608]{1,0:T(8,128)(2,1)}) %reduce-scatter.21.cloned.1.call-update) | async-done | bytes 1327120 | tf_op jit(solution)/shard_map/reduce_scatter | solution.py:264
  1015.4 85.6 %reduce-scatter.15.cloned.1.call-done = bf16[576,1152]{1,0:T(8,128)(2,1)} async-done(((bf16[4608,1152]{1,0:T(8,128)(2,1)}), bf16[576,1152]{1,0:T(8,128)(2,1)}) %reduce-scatter.15.cloned.1.call-update) | async-done | bytes 1327120 | tf_op jit(solution)/shard_map/reduce_scatter | solution.py:264
  1101.0 85.6 %reduce-scatter.13.cloned.1.call-done = bf16[144,4608]{1,0:T(8,128)(2,1)} async-done(((bf16[1152,4608]{1,0:T(8,128)(2,1)}), bf16[144,4608]{1,0:T(8,128)(2,1)}) %reduce-scatter.13.cloned.1.call-update) | async-done | bytes 1327120 | tf_op jit(solution)/shard_map/reduce_scatter | solution.py:264
  1191.4 19.3 %all_to_all.16 = bf16[8,1,4,1,16,1152]{5,4,2,3,1,0:T(8,128)(2,1)S(1)} all-to-all(bf16[8,1,4,1,16,1152]{5,4,2,3,1,0:T(8,128)(2,1)S(1)} %bitcast.348), channel_id=1, replica_groups=mesh['rep'=4,'seq'=8] {'seq'}, dimensions={0} | all-to-all | bytes 2359296 | tf_op jit(solution)/shard_map/all_to_all | solution.py:114
  1217.3 386.7 %all-reduce.5.cloned.1.call-done = (bf16[144,6912]{1,0:T(8,128)(2,1)}, bf16[144,3456]{1,0:T(8,128)(2,1)}, bf16[144,1152]{1,0:T(8,128)(2,1)}, bf16[144,4608]{1,0:...) async-done(((bf16[144,6912]{1,0:T(8,128)(2,1)}, ...) | async-done | bytes 11943952 | tf_op jit(solution)/shard_map/psum | solution.py:344
  (435 shorter events, 340.9 us)
Async XLA Ops:
  7.2 58.4 %all-gather.9.cloned.1.call-start = ((), (), s32[]{:S(2)}) async-start(), calls=%async_computation.12 | async-start | bytes 8957952 | tf_op jit(solution)/shard_map/all_gather | solution.py:64
  7.9 123.3 %all-gather.11.cloned.1.call-start = ((), (), s32[]{:S(2)}) async-start(), calls=%async_computation.13 | async-start | bytes 2985984 | tf_op jit(solution)/shard_map/all_gather | solution.py:65
  8.7 166.4 %all-gather.13.cloned.1.call-start = ((), (), s32[]{:S(2)}) async-start(), calls=%async_computation.14 | async-start | bytes 11943936 | tf_op jit(solution)/shard_map/all_gather | solution.py:66
  9.4 231.3 %all-gather.15.cloned.1.call-start = ((), (), s32[]{:S(2)}) async-start(), calls=%async_computation.15 | async-start | bytes 11943936 | tf_op jit(solution)/shard_map/all_gather | solution.py:67
  10.0 290.4 %all-gather.17.cloned.1.call-start = ((), (), s32[]{:S(2)}) async-start(), calls=%async_computation.16 | async-start | bytes 8957952 | tf_op jit(solution)/shard_map/all_gather | solution.py:64
  10.6 344.4 %all-gather.19.cloned.1.call-start = ((), (), s32[]{:S(2)}) async-start(), calls=%async_computation.17 | async-start | bytes 2985984 | tf_op jit(solution)/shard_map/all_gather | solution.py:65
  11.2 386.8 %all-gather.21.cloned.1.call-start = ((), (), s32[]{:S(2)}) async-start(), calls=%async_computation.18 | async-start | bytes 11943936 | tf_op jit(solution)/shard_map/all_gather | solution.py:66
  11.9 451.7 %all-gather.23.cloned.1.call-start = ((), (), s32[]{:S(2)}) async-start(), calls=%async_computation.19 | async-start | bytes 11943936 | tf_op jit(solution)/shard_map/all_gather | solution.py:67
  44.6 86.6 %copy-start.49 = (f32[1152]{0:T(1024)}, f32[1152]{0:T(1024)S(1)}, u32[]{:S(2)}) copy-start(f32[1152]{0:T(1024)S(1)} %get-tuple-element.36) | copy-start | bytes 13828
  44.6 130.5 %copy-start.55 = (f32[1152]{0:T(1024)}, f32[1152]{0:T(1024)S(1)}, u32[]{:S(2)}) copy-start(f32[1152]{0:T(1024)S(1)} %get-tuple-element.33) | copy-start | bytes 13828
  44.6 130.5 %copy-start.94 = (f32[1152]{0:T(1024)}, f32[1152]{0:T(1024)S(1)}, u32[]{:S(2)}) copy-start(f32[1152]{0:T(1024)S(1)} %get-tuple-element.32) | copy-start | bytes 13828
  44.6 196.1 %copy-start.63 = (f32[1152]{0:T(1024)}, f32[1152]{0:T(1024)S(1)}, u32[]{:S(2)}) copy-start(f32[1152]{0:T(1024)S(1)} %get-tuple-element.31) | copy-start | bytes 13828
  78.1 13.9 collective-permute-start
  80.2 175.4 %all-to-all-start.2 = ((bf16[1,1,4,8,16,1152]{5,4,2,1,0,3:T(8,128)(2,1)}), bf16[1,1,4,8,16,1152]{5,4,2,1,0,3:T(8,128)(2,1)}, u32[]{:S(2)}, u32[]{:S(2)}) async-start(bf16[1,1,4,8,16,1152]{5,4,2,1,0,3:T(8,128)(2,1)} %copy.281), calls=%async_computation.2 | async-start | bytes 2359296 | tf_op jit(solution)/shard_map/all_to_all | solution.py:92
  136.8 62.3 %copy-start.73 = (f32[4,128]{1,0:T(4,128)}, f32[4,128]{1,0:T(4,128)S(1)}, u32[]{:S(2)}) copy-start(f32[4,128]{1,0:T(4,128)S(1)} %broadcast_multiply_fusion.2) | copy-start | bytes 6148
  255.6 21.5 %all-to-all-start = ((bf16[1,1,4,8,16,1152]{5,4,2,1,0,3:T(8,128)(2,1)}), bf16[1,1,4,8,16,1152]{5,4,2,1,0,3:T(8,128)(2,1)S(1)}, u32[]{:S(2)}, u32[]{:S(2)}) async-start(bf16[1,1,4,8,16,1152]{5,4,2,1,0,3:T(8,128)(2,1)} %copy.260), calls=%async_computation | async-start | bytes 2359296 | tf_op jit(solution)/shard_map/all_to_all | solution.py:92
  259.3 138.6 %copy-start.98 = (f32[1152]{0:T(1024)}, f32[1152]{0:T(1024)S(1)}, u32[]{:S(2)}) copy-start(f32[1152]{0:T(1024)S(1)} %get-tuple-element.26) | copy-start | bytes 13828
  259.3 238.2 %copy-start.66 = (f32[1152]{0:T(1024)}, f32[1152]{0:T(1024)S(1)}, u32[]{:S(2)}) copy-start(f32[1152]{0:T(1024)S(1)} %get-tuple-element.27) | copy-start | bytes 13828
  259.3 238.2 %copy-start.68 = (f32[1152]{0:T(1024)}, f32[1152]{0:T(1024)S(1)}, u32[]{:S(2)}) copy-start(f32[1152]{0:T(1024)S(1)} %get-tuple-element.25) | copy-start | bytes 13828
  361.7 135.8 %copy-start.51 = (f32[32,16]{1,0:T(8,128)}, f32[32,16]{1,0:T(8,128)S(1)}, u32[]{:S(2)}) copy-start(f32[32,16]{1,0:T(8,128)S(1)} %copy.275) | copy-start | bytes 6148
  363.9 133.6 %copy-start.61 = (f32[32,16]{1,0:T(8,128)}, f32[32,16]{1,0:T(8,128)S(1)}, u32[]{:S(2)}) copy-start(f32[32,16]{1,0:T(8,128)S(1)} %copy.277) | copy-start | bytes 6148
  586.0 20.3 %all-to-all-start.3 = ((bf16[8,1,4,1,16,1152]{5,4,2,3,1,0:T(8,128)(2,1)}), bf16[8,1,4,1,16,1152]{5,4,2,3,1,0:T(8,128)(2,1)S(1)}, u32[]{:S(2)}, u32[]{:S(2)}) async-start(bf16[8,1,4,1,16,1152]{5,4,2,3,1,0:T(8,128)(2,1)} %bitcast.346), calls=%async_computation.3 | async-start | bytes 2359296 | tf_op jit(solution)/shard_map/all_to_all | solution.py:114
  589.5 234.3 %reduce-scatter.19.cloned.1.call-start = ((), (), s32[]{:S(2)}) async-start(), calls=%async_computation.25 | async-start | bytes 2985984 | tf_op jit(solution)/shard_map/reduce_scatter | solution.py:264
  602.3 221.5 %reduce-scatter.11.cloned.1.call-start = ((), (), s32[]{:S(2)}) async-start(), calls=%async_computation.21 | async-start | bytes 2985984 | tf_op jit(solution)/shard_map/reduce_scatter | solution.py:264
  645.7 178.1 %reduce-scatter.17.cloned.1.call-start = ((), (), s32[]{:S(2)}) async-start(), calls=%async_computation.24 | async-start | bytes 8957952 | tf_op jit(solution)/shard_map/reduce_scatter | solution.py:264
  657.0 187.1 %reduce-scatter.9.cloned.1.call-start = ((), (), s32[]{:S(2)}) async-start(), calls=%async_computation.20 | async-start | bytes 8957952 | tf_op jit(solution)/shard_map/reduce_scatter | solution.py:264
  703.0 5.3 collective-permute-start.1
  730.9 199.0 %reduce-scatter.23.cloned.1.call-start = ((), (), s32[]{:S(2)}) async-start(), calls=%async_computation.27 | async-start | bytes 11943936 | tf_op jit(solution)/shard_map/reduce_scatter | solution.py:264
  745.1 270.3 %reduce-scatter.21.cloned.1.call-start = ((), (), s32[]{:S(2)}) async-start(), calls=%async_computation.26 | async-start | bytes 11943936 | tf_op jit(solution)/shard_map/reduce_scatter | solution.py:264
  757.0 344.0 %reduce-scatter.15.cloned.1.call-start = ((), (), s32[]{:S(2)}) async-start(), calls=%async_computation.23 | async-start | bytes 11943936 | tf_op jit(solution)/shard_map/reduce_scatter | solution.py:264
  770.6 416.0 %reduce-scatter.13.cloned.1.call-start = ((), (), s32[]{:S(2)}) async-start(), calls=%async_computation.22 | async-start | bytes 11943936 | tf_op jit(solution)/shard_map/reduce_scatter | solution.py:264
  782.9 821.1 %all-reduce.5.cloned.1.call-start = ((), (), s32[]{:S(2)}) async-start(), calls=%async_computation.28 | async-start | bytes 23887872 | tf_op jit(solution)/shard_map/psum | solution.py:344
  (99 other events, 746.2 us)
Sparse Core Ops, SparseCore 0:
  9.9 55.5 all-gather.8
  67.4 38.6 all-gather.10
  108.1 66.9 all-gather.12
  176.8 63.8 all-gather.14
  242.4 57.9 all-gather.16
  302.2 29.9 all-gather.18
  334.1 63.8 all-gather.20
  399.8 63.8 all-gather.22
  602.4 45.0 reduce-scatter.18
  651.8 43.7 reduce-scatter.10
  699.2 70.5 reduce-scatter.16
  773.5 70.5 reduce-scatter.8
  847.6 82.1 reduce-scatter.22
  933.2 82.2 reduce-scatter.20
  1018.8 82.2 reduce-scatter.14
  1104.4 82.2 reduce-scatter.12
  1191.6 412.4 all-reduce.4
where the time goes:
time: 1640 us; the launch traced here: 1630 us
  waiting for transfers between devices  963 us (59%)
  matrix products  338 us (21%)
  local copies, waits for them, and re-layouts  141 us (9%)
  other arithmetic  90 us (5%)
  blocking collectives  69.6 us (4%)
    psum x1, waiting for transfers between devices, per_device(): lax.psum(mod_weight_one.astype(jnp.bfloat16), 'rep').astype(jnp.float32)  387 us
    reduce_scatter x8, waiting for transfers between devices, spread_rows_out(): lax.psum_scatter(jnp.einsum('nd,ne->de', left_flat, right_flat, preferred...  363 us
    dot_general x8, matrix products, project(): jnp.einsum('csld,de->csle', left_operand, right_operand, preferred_elemen...  99 us
    all_gather x2, waiting for transfers between devices, gather_layer(): lax.all_gather(down_w, 'seq', axis=0, tiled=True)  94.2 us
    dot_general x8, matrix products, project_back(): jnp.einsum('csle,de->csld', incoming, right_operand, preferred_element_ty...  87.1 us
    dot_general x8, matrix products, spread_rows_out(): jnp.einsum('nd,ne->de', left_flat, right_flat, preferred_element_type=jnp...  76.2 us
    all_gather x2, waiting for transfers between devices, gather_layer(): lax.all_gather(up_w, 'seq', axis=0, tiled=True)  70.6 us
  transfers between devices with their start and end apart: 22, of which 14 were waited for; matrix products, arithmetic and copies ran while one was open for 25% of the time, Pallas kernels for 0%

commit v1 on v0

--- a/solution.py
+++ b/solution.py
@@ -340,8 +340,12 @@
     )
     condition_local = lax.dynamic_slice_in_dim(conditioning, row_start, row_attn, 1)
     condition_grad = jax.vjp(jax.nn.silu, condition_local)[1](silu_grad)[0]
+
+    def _choose_block(view, net_axis):
+        return jnp.sum(jax.lax.all_gather(view, net_axis), axis=0)
+
     summed = (
-        lax.psum(mod_weight_one.astype(jnp.bfloat16), "rep").astype(jnp.float32),
+        _choose_block(mod_weight_one.astype(jnp.bfloat16), "rep").astype(jnp.float32),
         lax.psum(grads_one[0].astype(jnp.bfloat16), "rep").astype(jnp.float32),
         lax.psum(grads_one[1].astype(jnp.bfloat16), "rep").astype(jnp.float32),
         lax.psum(grads_one[2].astype(jnp.bfloat16), "rep").astype(jnp.float32),

time: 1640 us -> 1710 us (1.043)
  waiting for transfers between devices: 963 us -> 1030 us
    all_gather x0 -> x1, waiting for transfers between devices: none -> 114 us  [_choose_block(): return jnp.sum(jax.lax.all_gather(view, net_axis), axis=0)]
    psum x1, waiting for transfers between devices: 387 us -> 339 us  [per_device(): lax.psum(grads_one[0].astype(jnp.bfloat16), 'rep').astype(jnp.float32)]
  transfers between devices with their start and end apart: 22 -> 23, of which waited for: 14 -> 15; matrix products, arithmetic and copies ran while one was open for 25% -> 25% of each run, Pallas kernels for 0% -> 0%
where the time goes in v1:
time: 1710 us; the launch traced here: 1700 us
  waiting for transfers between devices  1030 us (60%)
  matrix products  338 us (20%)
  local copies, waits for them, and re-layouts  141 us (8%)
  other arithmetic  97.8 us (6%)
  blocking collectives  69.4 us (4%)
    reduce_scatter x8, waiting for transfers between devices, spread_rows_out(): lax.psum_scatter(jnp.einsum('nd,ne->de', left_flat, right_flat, preferred...  363 us
    psum x1, waiting for transfers between devices, per_device(): lax.psum(grads_one[0].astype(jnp.bfloat16), 'rep').astype(jnp.float32)  339 us
    all_gather x1, waiting for transfers between devices, _choose_block(): return jnp.sum(jax.lax.all_gather(view, net_axis), axis=0)  114 us
    dot_general x8, matrix products, project(): jnp.einsum('csld,de->csle', left_operand, right_operand, preferred_elemen...  98.9 us
    all_gather x2, waiting for transfers between devices, gather_layer(): lax.all_gather(down_w, 'seq', axis=0, tiled=True)  94.3 us
    dot_general x8, matrix products, project_back(): jnp.einsum('csle,de->csld', incoming, right_operand, preferred_element_ty...  87.1 us
    dot_general x8, matrix products, spread_rows_out(): jnp.einsum('nd,ne->de', left_flat, right_flat, preferred_element_type=jnp...  76.1 us
    all_gather x2, waiting for transfers between devices, gather_layer(): lax.all_gather(up_w, 'seq', axis=0, tiled=True)  70.7 us
  transfers between devices with their start and end apart: 23, of which 15 were waited for; matrix products, arithmetic and copies ran while one was open for 25% of the time, Pallas kernels for 0%

profile of v1, /device:TPU:0, one launch (start us, length us, event | category | flops | bytes accessed | tf_op | source)
XLA Modules:
  0.0 1704.5 jit_solution(6959654916004957153)
XLA Ops:
  17.6 26.8 %all-reduce = (f32[1,6912]{1,0:T(1,128)S(1)}, f32[1,6912]{1,0:T(1,128)S(1)}) all-reduce(f32[1,6912]{1,0:T(1,128)S(1)} %fusion.149, f32[1,6912]{1,0:T(1,128)S(1)} %fusion.147), channel_id=1, replica_groups=mesh['rep'=4,'seq'=8] {'seq'}, use_global_device_ids=true, to_apply=%region_0.1 | all-reduce | flops 13824 | bytes 110592 | tf_op jit(solution)/shard_map/psum | solution.py:58
  44.6 21.0 %all-gather.11.cloned.1.call-done = bf16[1152,3456]{1,0:T(8,128)(2,1)} async-done(((bf16[144,3456]{1,0:T(8,128)(2,1)}), bf16[1152,3456]{1,0:T(8,128)(2,1)}) %all-gather.11.cloned.1.call-update) | async-done | bytes 7962640 | tf_op jit(solution)/shard_map/all_gather | solution.py:64
  109.1 22.0 %fusion.119 = bf16[4,16,72,128]{3,2,1,0:T(8,128)(2,1)} fusion(bf16[1,4,128,16,72]{2,4,3,1,0:T(8,128)(2,1)} %bitcast.358, bf16[1,4,128,16,72]{2,4,3,1,0:T(8,128)(2,1)} %bitcast.356, f32[4,16,128]{2,1,0:T(8,128)S(1)} %get-tuple-element.80, f32[4,16,128,256]{3,2,1,0:T(8,128)} %copy-done.5), kind=kOutput, calls=%fused_computation.180 | convolution fusion | flops 317792512 | bytes 11960320 | tf_op jit(solution)/shard_map/cshlm,csmhe->cslhe/dot_general | solution.py:142
  138.5 36.6 %all-gather.15.cloned.1.call-done = bf16[1152,4608]{1,0:T(8,128)(2,1)} async-done(((bf16[144,4608]{1,0:T(8,128)(2,1)}), bf16[1152,4608]{1,0:T(8,128)(2,1)}) %all-gather.15.cloned.1.call-update) | async-done | bytes 10616848 | tf_op jit(solution)/shard_map/all_gather | solution.py:66
  175.1 23.9 %fusion.22 = f32[4,128,4608]{2,1,0:T(8,128)} fusion(bf16[1152,4608]{1,0:T(8,128)(2,1)} %all-gather.15.cloned.1.call-done, f32[4,128,1152]{2,1,0:T(8,128)} %copy-done.3, f32[1152]{0:T(1024)S(1)} %get-tuple-element.32, f32[1152]{0:T(1024)S(1)} %get-tuple-element.33, f32[4,128]{1,0:T(4,128)S(1)} %fusion.144, f32[4,128]{1,0:T(4,128)S(1)} %broadcast_multiply_fusion.2), kind=kOutput, calls=%fused_computation.32 | convolution fusion | flops 5438767104 | bytes 22426624 | tf_op jit(solution)/shard_map/csld,de->csle/dot_general | solution.py:37
  199.0 41.7 %all-gather.17.cloned.1.call-done = bf16[4608,1152]{1,0:T(8,128)(2,1)} async-done(((bf16[576,1152]{1,0:T(8,128)(2,1)}), bf16[4608,1152]{1,0:T(8,128)(2,1)}) %all-gather.17.cloned.1.call-update) | async-done | bytes 10616848 | tf_op jit(solution)/shard_map/all_gather | solution.py:67
  240.7 13.8 add_convert_fusion.4
  330.9 16.3 fusion.179
  363.8 34.1 %all-gather.23.cloned.1.call-done = bf16[1152,4608]{1,0:T(8,128)(2,1)} async-done(((bf16[144,4608]{1,0:T(8,128)(2,1)}), bf16[1152,4608]{1,0:T(8,128)(2,1)}) %all-gather.23.cloned.1.call-update) | async-done | bytes 10616848 | tf_op jit(solution)/shard_map/all_gather | solution.py:66
  397.9 13.2 fusion.14
  411.1 52.6 %all-gather.25.cloned.1.call-done = bf16[4608,1152]{1,0:T(8,128)(2,1)} async-done(((bf16[576,1152]{1,0:T(8,128)(2,1)}), bf16[4608,1152]{1,0:T(8,128)(2,1)}) %all-gather.25.cloned.1.call-update) | async-done | bytes 10616848 | tf_op jit(solution)/shard_map/all_gather | solution.py:67
  463.7 15.9 fusion.37
  479.6 13.5 multiply_reduce_fusion.13
  497.5 18.1 %multiply_reduce_fusion.4 = (bf16[1152]{0:T(1024)(128)(2,1)}, bf16[32,16,1152]{2,1,0:T(8,128)(2,1)}, bf16[1152]{0:T(1024)(128)(2,1)}, f32[32,16,1152]{2,1,0:T(8,128)S(1)}) fusion(f32[32,16,1152]{2,1,0:T(8,128)} %reshape.1279, f32[32,16,1152]{2,1,0:T(8,128)} %get-tuple-element.58, f32[1152]{0:T(1024)S(1)} %get-tuple-element.25, ...), kind=kOutput, calls=%fused_computation.133 | convolution fusion | flops 5465896960 | bytes 33052160 | tf_op jit(solution)/shard_map/csld,de->csle/dot_general | solution.py:37
  563.1 10.9 multiply_reduce_fusion.12
  606.5 17.4 %fusion.30 = bf16[4,128,4608]{2,1,0:T(8,128)(2,1)} fusion(f32[4,128,4608]{2,1,0:T(8,128)} %fusion.22, bf16[4608,1152]{1,0:T(8,128)(2,1)} %all-gather.17.cloned.1.call-done, f32[4,128,1152]{2,1,0:T(8,128)S(1)} %bitcast.338, f32[1152]{0:T(1024)S(1)} %copy-done.63), kind=kOutput, calls=%fused_computation.40 | convolution fusion | flops 5484183552 | bytes 27136512 | tf_op jit(solution)/shard_map/csle,de->csld/dot_general | solution.py:43
  623.9 11.9 multiply_reduce_fusion.11
  664.3 22.3 %convolution_bitcast_fusion.6 = f32[1,4,256,16,72]{2,4,3,1,0:T(8,128)} fusion(bf16[4,128,16,72]{1,3,2,0:T(8,128)(2,1)} %bitcast.362, f32[4,16,128]{2,1,0:T(8,128)S(1)} %copy-done.53, f32[4,16,128,256]{3,2,1,0:T(8,128)} %copy-done.5), kind=kOutput, calls=%fused_computation.161 | convolution fusion | flops 312484096 | bytes 14319616 | tf_op jit(solution)/shard_map/cshlm,cslhe->csmhe/dot_general | solution.py:219
  732.1 12.9 fusion.3
  745.8 11.1 fusion.2
  758.3 12.1 fusion.5
  771.2 11.5 fusion.4
  784.0 10.9 fusion.85
  797.7 23.3 %all-reduce.1 = (bf16[6912]{0:T(1024)(128)(2,1)S(1)}, bf16[6912]{0:T(1024)(128)(2,1)S(1)}) all-reduce(bf16[6912]{0:T(1024)(128)(2,1)S(1)} %reduce.80, bf16[6912]{0:T(1024)(128)(2,1)S(1)} %reduce.81), channel_id=1, replica_groups=mesh['rep'=4,'seq'=8] {'seq'}, use_global_device_ids=true, to_apply=%region_30.31 | all-reduce | flops 13824 | bytes 55296 | tf_op jit(solution)/shard_map/psum | solution.py:326
  823.8 20.2 %reduce-scatter.9.cloned.1.call-done = bf16[144,3456]{1,0:T(8,128)(2,1)} async-done(((bf16[1152,3456]{1,0:T(8,128)(2,1)}), bf16[144,3456]{1,0:T(8,128)(2,1)}) %reduce-scatter.9.cloned.1.call-update) | async-done | bytes 995344 | tf_op jit(solution)/shard_map/reduce_scatter | solution.py:264
  844.0 85.8 %reduce-scatter.23.cloned.1.call-done = bf16[576,1152]{1,0:T(8,128)(2,1)} async-done(((bf16[4608,1152]{1,0:T(8,128)(2,1)}), bf16[576,1152]{1,0:T(8,128)(2,1)}) %reduce-scatter.23.cloned.1.call-update) | async-done | bytes 1327120 | tf_op jit(solution)/shard_map/reduce_scatter | solution.py:264
  929.8 85.6 %reduce-scatter.21.cloned.1.call-done = bf16[144,4608]{1,0:T(8,128)(2,1)} async-done(((bf16[1152,4608]{1,0:T(8,128)(2,1)}), bf16[144,4608]{1,0:T(8,128)(2,1)}) %reduce-scatter.21.cloned.1.call-update) | async-done | bytes 1327120 | tf_op jit(solution)/shard_map/reduce_scatter | solution.py:264
  1015.4 85.6 %reduce-scatter.15.cloned.1.call-done = bf16[576,1152]{1,0:T(8,128)(2,1)} async-done(((bf16[4608,1152]{1,0:T(8,128)(2,1)}), bf16[576,1152]{1,0:T(8,128)(2,1)}) %reduce-scatter.15.cloned.1.call-update) | async-done | bytes 1327120 | tf_op jit(solution)/shard_map/reduce_scatter | solution.py:264
  1101.0 85.6 %reduce-scatter.13.cloned.1.call-done = bf16[144,4608]{1,0:T(8,128)(2,1)} async-done(((bf16[1152,4608]{1,0:T(8,128)(2,1)}), bf16[144,4608]{1,0:T(8,128)(2,1)}) %reduce-scatter.13.cloned.1.call-update) | async-done | bytes 1327120 | tf_op jit(solution)/shard_map/reduce_scatter | solution.py:264
  1191.3 19.3 %all_to_all.16 = bf16[8,1,4,1,16,1152]{5,4,2,3,1,0:T(8,128)(2,1)S(1)} all-to-all(bf16[8,1,4,1,16,1152]{5,4,2,3,1,0:T(8,128)(2,1)S(1)} %bitcast.350), channel_id=1, replica_groups=mesh['rep'=4,'seq'=8] {'seq'}, dimensions={0} | all-to-all | bytes 2359296 | tf_op jit(solution)/shard_map/all_to_all | solution.py:114
  1217.2 114.1 %all-gather.27.cloned.1.call-done = bf16[576,6912]{1,0:T(8,128)(2,1)} async-done(((bf16[144,6912]{1,0:T(8,128)(2,1)}), bf16[576,6912]{1,0:T(8,128)(2,1)}) %all-gather.27.cloned.1.call-update) | async-done | bytes 7962640 | tf_op jit(solution)/shard_map/all_gather | solution.py:345
  1341.3 339.4 %all-reduce.5.cloned.1.call-done = (bf16[144,3456]{1,0:T(8,128)(2,1)}, bf16[144,1152]{1,0:T(8,128)(2,1)}, bf16[144,4608]{1,0:T(8,128)(2,1)}, bf16[576,1152]{1,0:...) async-done(((bf16[144,3456]{1,0:T(8,128)(2,1)}, ...) | async-done | bytes 9953296 | tf_op jit(solution)/shard_map/psum | solution.py:349
  (437 shorter events, 359.5 us)
Async XLA Ops:
  7.2 58.4 %all-gather.11.cloned.1.call-start = ((), (), s32[]{:S(2)}) async-start(), calls=%async_computation.12 | async-start | bytes 8957952 | tf_op jit(solution)/shard_map/all_gather | solution.py:64
  7.9 123.2 %all-gather.13.cloned.1.call-start = ((), (), s32[]{:S(2)}) async-start(), calls=%async_computation.13 | async-start | bytes 2985984 | tf_op jit(solution)/shard_map/all_gather | solution.py:65
  8.7 166.4 %all-gather.15.cloned.1.call-start = ((), (), s32[]{:S(2)}) async-start(), calls=%async_computation.14 | async-start | bytes 11943936 | tf_op jit(solution)/shard_map/all_gather | solution.py:66
  9.4 231.2 %all-gather.17.cloned.1.call-start = ((), (), s32[]{:S(2)}) async-start(), calls=%async_computation.15 | async-start | bytes 11943936 | tf_op jit(solution)/shard_map/all_gather | solution.py:67
  10.0 290.4 %all-gather.19.cloned.1.call-start = ((), (), s32[]{:S(2)}) async-start(), calls=%async_computation.16 | async-start | bytes 8957952 | tf_op jit(solution)/shard_map/all_gather | solution.py:64
  10.6 344.3 %all-gather.21.cloned.1.call-start = ((), (), s32[]{:S(2)}) async-start(), calls=%async_computation.17 | async-start | bytes 2985984 | tf_op jit(solution)/shard_map/all_gather | solution.py:65
  11.2 386.8 %all-gather.23.cloned.1.call-start = ((), (), s32[]{:S(2)}) async-start(), calls=%async_computation.18 | async-start | bytes 11943936 | tf_op jit(solution)/shard_map/all_gather | solution.py:66
  11.9 451.7 %all-gather.25.cloned.1.call-start = ((), (), s32[]{:S(2)}) async-start(), calls=%async_computation.19 | async-start | bytes 11943936 | tf_op jit(solution)/shard_map/all_gather | solution.py:67
  44.6 86.6 %copy-start.48 = (f32[1152]{0:T(1024)}, f32[1152]{0:T(1024)S(1)}, u32[]{:S(2)}) copy-start(f32[1152]{0:T(1024)S(1)} %get-tuple-element.36) | copy-start | bytes 13828
  44.6 130.5 %copy-start.54 = (f32[1152]{0:T(1024)}, f32[1152]{0:T(1024)S(1)}, u32[]{:S(2)}) copy-start(f32[1152]{0:T(1024)S(1)} %get-tuple-element.33) | copy-start | bytes 13828
  44.6 130.5 %copy-start.93 = (f32[1152]{0:T(1024)}, f32[1152]{0:T(1024)S(1)}, u32[]{:S(2)}) copy-start(f32[1152]{0:T(1024)S(1)} %get-tuple-element.32) | copy-start | bytes 13828
  44.6 196.1 %copy-start.62 = (f32[1152]{0:T(1024)}, f32[1152]{0:T(1024)S(1)}, u32[]{:S(2)}) copy-start(f32[1152]{0:T(1024)S(1)} %get-tuple-element.31) | copy-start | bytes 13828
  78.1 14.0 collective-permute-start
  80.2 175.4 %all-to-all-start.2 = ((bf16[1,1,4,8,16,1152]{5,4,2,1,0,3:T(8,128)(2,1)}), bf16[1,1,4,8,16,1152]{5,4,2,1,0,3:T(8,128)(2,1)}, u32[]{:S(2)}, u32[]{:S(2)}) async-start(bf16[1,1,4,8,16,1152]{5,4,2,1,0,3:T(8,128)(2,1)} %copy.281), calls=%async_computation.2 | async-start | bytes 2359296 | tf_op jit(solution)/shard_map/all_to_all | solution.py:92
  255.6 21.5 %all-to-all-start = ((bf16[1,1,4,8,16,1152]{5,4,2,1,0,3:T(8,128)(2,1)}), bf16[1,1,4,8,16,1152]{5,4,2,1,0,3:T(8,128)(2,1)S(1)}, u32[]{:S(2)}, u32[]{:S(2)}) async-start(bf16[1,1,4,8,16,1152]{5,4,2,1,0,3:T(8,128)(2,1)} %copy.260), calls=%async_computation | async-start | bytes 2359296 | tf_op jit(solution)/shard_map/all_to_all | solution.py:92
  259.3 138.6 %copy-start.97 = (f32[1152]{0:T(1024)}, f32[1152]{0:T(1024)S(1)}, u32[]{:S(2)}) copy-start(f32[1152]{0:T(1024)S(1)} %get-tuple-element.26) | copy-start | bytes 13828
  259.3 238.2 %copy-start.65 = (f32[1152]{0:T(1024)}, f32[1152]{0:T(1024)S(1)}, u32[]{:S(2)}) copy-start(f32[1152]{0:T(1024)S(1)} %get-tuple-element.27) | copy-start | bytes 13828
  259.3 238.1 %copy-start.67 = (f32[1152]{0:T(1024)}, f32[1152]{0:T(1024)S(1)}, u32[]{:S(2)}) copy-start(f32[1152]{0:T(1024)S(1)} %get-tuple-element.25) | copy-start | bytes 13828
  361.6 135.8 %copy-start.50 = (f32[32,16]{1,0:T(8,128)}, f32[32,16]{1,0:T(8,128)S(1)}, u32[]{:S(2)}) copy-start(f32[32,16]{1,0:T(8,128)S(1)} %copy.275) | copy-start | bytes 6148
  363.8 133.6 %copy-start.60 = (f32[32,16]{1,0:T(8,128)}, f32[32,16]{1,0:T(8,128)S(1)}, u32[]{:S(2)}) copy-start(f32[32,16]{1,0:T(8,128)S(1)} %copy.277) | copy-start | bytes 6148
  586.0 20.3 %all-to-all-start.3 = ((bf16[8,1,4,1,16,1152]{5,4,2,3,1,0:T(8,128)(2,1)}), bf16[8,1,4,1,16,1152]{5,4,2,3,1,0:T(8,128)(2,1)S(1)}, u32[]{:S(2)}, u32[]{:S(2)}) async-start(bf16[8,1,4,1,16,1152]{5,4,2,3,1,0:T(8,128)(2,1)} %bitcast.348), calls=%async_computation.3 | async-start | bytes 2359296 | tf_op jit(solution)/shard_map/all_to_all | solution.py:114
  589.5 234.2 %reduce-scatter.19.cloned.1.call-start = ((), (), s32[]{:S(2)}) async-start(), calls=%async_computation.25 | async-start | bytes 2985984 | tf_op jit(solution)/shard_map/reduce_scatter | solution.py:264
  602.3 221.5 %reduce-scatter.11.cloned.1.call-start = ((), (), s32[]{:S(2)}) async-start(), calls=%async_computation.21 | async-start | bytes 2985984 | tf_op jit(solution)/shard_map/reduce_scatter | solution.py:264
  645.6 178.2 %reduce-scatter.17.cloned.1.call-start = ((), (), s32[]{:S(2)}) async-start(), calls=%async_computation.24 | async-start | bytes 8957952 | tf_op jit(solution)/shard_map/reduce_scatter | solution.py:264
  656.9 187.1 %reduce-scatter.9.cloned.1.call-start = ((), (), s32[]{:S(2)}) async-start(), calls=%async_computation.20 | async-start | bytes 8957952 | tf_op jit(solution)/shard_map/reduce_scatter | solution.py:264
  703.0 5.3 collective-permute-start.1
  730.8 198.9 %reduce-scatter.23.cloned.1.call-start = ((), (), s32[]{:S(2)}) async-start(), calls=%async_computation.27 | async-start | bytes 11943936 | tf_op jit(solution)/shard_map/reduce_scatter | solution.py:264
  745.1 270.3 %reduce-scatter.21.cloned.1.call-start = ((), (), s32[]{:S(2)}) async-start(), calls=%async_computation.26 | async-start | bytes 11943936 | tf_op jit(solution)/shard_map/reduce_scatter | solution.py:264
  756.9 344.1 %reduce-scatter.15.cloned.1.call-start = ((), (), s32[]{:S(2)}) async-start(), calls=%async_computation.23 | async-start | bytes 11943936 | tf_op jit(solution)/shard_map/reduce_scatter | solution.py:264
  770.5 416.1 %reduce-scatter.13.cloned.1.call-start = ((), (), s32[]{:S(2)}) async-start(), calls=%async_computation.22 | async-start | bytes 11943936 | tf_op jit(solution)/shard_map/reduce_scatter | solution.py:264
  782.7 548.5 %all-gather.27.cloned.1.call-start = ((), (), s32[]{:S(2)}) async-start(), calls=%async_computation.28 | async-start | bytes 9953280 | tf_op jit(solution)/shard_map/all_gather | solution.py:345
  823.5 857.3 %all-reduce.5.cloned.1.call-start = ((), (), s32[]{:S(2)}) async-start(), calls=%async_computation.29 | async-start | bytes 19906560 | tf_op jit(solution)/shard_map/psum | solution.py:349
  (99 other events, 809.5 us)
Sparse Core Ops, SparseCore 0:
  9.9 55.5 all-gather.10
  67.4 38.6 all-gather.12
  108.1 66.9 all-gather.14
  176.8 63.8 all-gather.16
  242.4 57.9 all-gather.18
  302.2 29.9 all-gather.20
  334.1 63.8 all-gather.22
  399.8 63.8 all-gather.24
  602.4 45.1 reduce-scatter.18
  651.9 43.7 reduce-scatter.10
  699.2 70.3 reduce-scatter.16
  773.5 70.5 reduce-scatter.8
  847.5 82.1 reduce-scatter.22
  933.1 82.2 reduce-scatter.20
  1018.7 82.1 reduce-scatter.14
  1104.3 82.2 reduce-scatter.12
  1188.6 142.6 all-gather.26
  1335.4 345.2 all-reduce.4
